TPU v7x, 32 devices: a whole 2x2x4 slice. The times are simulated.
32 devices in a mesh: gx: 4 (over y, x), gy: 8 (over z, core).
Axes of the slice: x: 2, y: 2, z: 4, core: 2. Of those that a mesh axis runs over, the one named last changes fastest.
Arguments:
- density_one: float32 [512, 512, 512], P('gx', 'gy'), may hold values from -6 to 6
- density_two: float32 [512, 512, 512], P('gx', 'gy'), may hold values from -6 to 6
Outputs:
- correlation: float32 [512, 512, 512], P('gx', 'gy')
All inputs are finite; a program needn't handle non-finite values.
Results may differ from a plain program's by a relative error of at most 0.00013.
Values sent between devices are 32-bit elements; how exact they have to be, the bound alone decides.
A program may use at most 256 MiB of HBM per device.

v0:
```python
import math

import jax
import jax.numpy as jnp
import numpy as np
from jax import lax
from jax.sharding import PartitionSpec as P

split_mode = lax.Precision.HIGH


def phases(numerator, denominator):
    radians = (numerator % denominator) * (2.0 * math.pi / denominator)
    return np.cos(radians), np.sin(radians)


def base_table(length):
    positions = np.arange(length)
    cosines, sines = phases(positions[:, None] * positions[None, :], length)
    return cosines.astype(np.float32), sines.astype(np.float32)


def complex_table(base, direction):
    cosines, sines = base
    signed = direction * sines
    real_rows = jnp.stack([cosines, signed], axis=1)
    imag_rows = jnp.stack([-signed, cosines], axis=1)
    return jnp.stack([real_rows, imag_rows], axis=0)


def depth_tables(depth_cells, devices, kz_slices, chunk, chunk_slices, scale):
    wave = (
        np.arange(devices)[:, None] * kz_slices
        + chunk * chunk_slices
        + np.arange(chunk_slices)[None, :]
    )
    cosines, sines = phases(wave[:, :, None] * np.arange(depth_cells), depth_cells)
    weight = np.where(wave == 0, 1.0, 2.0)[:, :, None] * scale
    forward = np.stack([cosines, -sines], axis=1).reshape(-1, depth_cells)
    inverse = np.stack([weight * cosines, -weight * sines], axis=1).reshape(-1, depth_cells)
    return forward.astype(np.float32), inverse.astype(np.float32)


def on_device(density_one, density_two):
    count_x = lax.axis_size("gx")
    count_y = lax.axis_size("gy")
    devices = count_x * count_y
    x_local, y_local, depth_cells = density_one.shape
    grid_x = x_local * count_x
    grid_y = y_local * count_y
    kz_slices = depth_cells // 2 // devices
    cell_total = float(grid_x * grid_y * depth_cells)
    chunks = 2 if kz_slices % 2 == 0 else 1
    per_chunk = kz_slices // chunks

    base_x = base_table(grid_x)
    base_y = base_x if grid_y == grid_x else base_table(grid_y)
    x_forward = complex_table(base_x, -1.0).reshape(2, count_x, x_local, 2, grid_x)
    x_inverse = complex_table(base_x, 1.0).reshape(2, grid_x, 2, count_x, x_local)
    y_forward = complex_table(base_y, -1.0).reshape(2, count_y, y_local, 2, grid_y)
    y_inverse = jnp.stack(base_y, axis=1).reshape(grid_y, 2, count_y, y_local)
    tables = [
        depth_tables(depth_cells, devices, kz_slices, chunk, per_chunk, 1.0 / math.sqrt(cell_total))
        for chunk in range(chunks)
    ]
    keep_x = np.arange(grid_x) != grid_x // 2
    keep_y = np.arange(grid_y) != grid_y // 2
    keep = keep_y[:, None, None] & keep_x[None, None, :]

    def exchange(rows):
        return lax.all_to_all(rows, ("gx", "gy"), split_axis=0, concat_axis=0, tiled=True)

    def product(pattern, left, right):
        return jnp.einsum(pattern, left, right, precision=split_mode)

    def depth_forward(density, table):
        lines = product("gz,xyz->gyx", table, density)
        return exchange(lines.reshape(devices, 2 * per_chunk, y_local * x_local))

    def plane_forward(rows):
        rows = rows.reshape(count_x, count_y, 2, per_chunk, y_local, x_local)
        lines = product("dspkyx,pdxrw->skyrw", rows, x_forward)
        return product("skyrw,rsytq->tqkw", lines, y_forward)

    moved = [
        [depth_forward(density, forward) for density in (density_one, density_two)]
        for forward, _ in tables
    ]
    correlation = None
    for (one, two), (_, inverse) in zip(moved, tables):
        first = plane_forward(one)
        second = plane_forward(two)
        power = (first[0] * second[0] + first[1] * second[1]) / cell_total
        power = jnp.where(keep, power, 0.0)
        lines = product("qkw,qrsy->srkyw", power, y_inverse)
        blocks = product("srkyw,rwpdx->dspkyx", lines, x_inverse)
        back = exchange(blocks.reshape(devices, 2 * per_chunk, y_local * x_local))
        back = back.reshape(devices * 2 * per_chunk, y_local, x_local)
        part = product("gyx,gz->xyz", back, inverse)
        correlation = part if correlation is None else correlation + part
    return correlation


def solution(mesh):
    return jax.shard_map(
        on_device,
        mesh=mesh,
        in_specs=(P("gx", "gy", None), P("gx", "gy", None)),
        out_specs=P("gx", "gy", None),
        check_vma=False,
    )
```

profile of v0, /device:TPU:0, one launch (start us, length us, event | category | flops | bytes accessed | tf_op | source)
XLA Modules:
  0.0 1237.3 jit_solution(255929885970680652)
XLA Ops:
  0.0 21.4 %fusion.56 = f32[256,64,128]{2,0,1:T(8,128)S(1)} fusion(f32[256,512,1]{1,0,2:T(8,128)} %constant.58, f32[128,64,512]{2,1,0:T(8,128)} %param.23), kind=kOutput, calls=%fused_computation.57 | convolution fusion | flops 6442450944 | bytes 25690112 | tf_op jit(solution)/shard_map/gz,xyz->gyx/dot_general | solution.py:74
  21.4 8.3 copy.93
  29.7 9.5 reshape.96
  39.1 7.6 all-to-all-start.3
  46.8 21.3 %fusion.53 = f32[256,64,128]{2,0,1:T(8,128)S(1)} fusion(f32[256,512,1]{1,0,2:T(8,128)S(1)} %copy-done.1, f32[128,64,512]{2,1,0:T(8,128)} %param.23), kind=kOutput, calls=%fused_computation.56 | convolution fusion | flops 6442450944 | bytes 25690112 | tf_op jit(solution)/shard_map/gz,xyz->gyx/dot_general | solution.py:74
  68.1 8.3 copy.85
  76.4 9.5 reshape.90
  85.8 145.7 %all-to-all-done.3 = f32[32,8,8192]{2,1,0:T(8,128)} async-done(((f32[32,8,8192]{2,1,0:T(8,128)}), f32[32,8,8192]{2,1,0:T(8,128)}, u32[]{:S(2)}, u32[]{:S(2)}) %all-to-all-start.3) | async-done | bytes 8388640 | tf_op jit(solution)/shard_map/all_to_all | solution.py:71
  231.5 3.9 all-to-all-start
  235.4 21.3 %fusion.62 = f32[256,64,128]{2,0,1:T(8,128)S(1)} fusion(f32[256,512,1]{1,0,2:T(8,128)S(1)} %copy-done.2, f32[128,64,512]{2,1,0:T(8,128)} %param.24), kind=kOutput, calls=%fused_computation.59 | convolution fusion | flops 6442450944 | bytes 25690112 | tf_op jit(solution)/shard_map/gz,xyz->gyx/dot_general | solution.py:74
  256.8 8.3 copy.96
  265.0 9.4 reshape.98
  274.4 145.8 %all-to-all-done = f32[32,8,8192]{2,1,0:T(8,128)} async-done(((f32[32,8,8192]{2,1,0:T(8,128)}), f32[32,8,8192]{2,1,0:T(8,128)}, u32[]{:S(2)}, u32[]{:S(2)}) %all-to-all-start) | async-done | bytes 8388640 | tf_op jit(solution)/shard_map/all_to_all | solution.py:71
  420.2 4.1 all-to-all-start.4
  424.3 21.3 %fusion.59 = f32[256,64,128]{2,0,1:T(8,128)S(1)} fusion(f32[256,512,1]{1,0,2:T(8,128)S(1)} %copy-done.1, f32[128,64,512]{2,1,0:T(8,128)} %param.24), kind=kOutput, calls=%fused_computation.58 | convolution fusion | flops 6442450944 | bytes 25690112 | tf_op jit(solution)/shard_map/gz,xyz->gyx/dot_general | solution.py:74
  445.6 8.3 copy.88
  453.9 9.4 reshape.92
  463.3 145.7 %all-to-all-done.4 = f32[32,8,8192]{2,1,0:T(8,128)} async-done(((f32[32,8,8192]{2,1,0:T(8,128)}), f32[32,8,8192]{2,1,0:T(8,128)}, u32[]{:S(2)}, u32[]{:S(2)}) %all-to-all-start.4) | async-done | bytes 8388640 | tf_op jit(solution)/shard_map/all_to_all | solution.py:71
  609.1 3.9 all-to-all-start.1
  613.1 5.0 copy.134
  618.1 5.2 copy.135
  623.3 13.9 %fusion.22 = f32[8,4,64,2,512,1,1]{4,2,6,1,0,3,5:T(8,128)S(1)} fusion(f32[2,4,128,2,512,1,1]{4,2,0,6,5,3,1:T(8,128)S(1)} %copy-done.8, f32[4,8,2,4,64,128,1]{5,4,3,2,1,0,6:T(8,128)S(1)} %bitcast.179), kind=kOutput, calls=%fused_computation.23 | convolution fusion | flops 12884901888 | bytes 20971520 | tf_op jit(solution)/shard_map/dspkyx,pdxrw->skyrw/dot_general | solution.py:74
  637.2 14.1 %fusion.20 = f32[8,4,64,2,512,1,1]{4,2,6,1,0,3,5:T(8,128)S(1)} fusion(f32[2,4,128,2,512,1,1]{4,2,0,6,5,3,1:T(8,128)S(1)} %copy-done.8, f32[4,8,2,4,64,128,1]{5,4,3,2,1,0,6:T(8,128)S(1)} %bitcast.180), kind=kOutput, calls=%fused_computation.21 | convolution fusion | flops 12884901888 | bytes 20971520 | tf_op jit(solution)/shard_map/dspkyx,pdxrw->skyrw/dot_general | solution.py:74
  651.3 15.3 %fusion.74 = f32[2,512,4,512]{3,1,2,0:T(8,128)S(1)} fusion(f32[2,8,64,2,512,1]{4,2,1,0,5,3:T(8,128)S(1)} %copy-done.6, f32[8,4,64,2,512,1,1]{4,2,6,1,0,3,5:T(8,128)S(1)} %fusion.22), kind=kOutput, calls=%fused_computation.63 | convolution fusion | flops 12884901888 | bytes 20971520 | tf_op jit(solution)/shard_map/skyrw,rsytq->tqkw/dot_general | solution.py:74
  666.6 16.2 %fusion.77 = f32[2,512,4,512]{3,1,2,0:T(8,128)} fusion(f32[2,8,64,2,512,1]{4,2,1,0,5,3:T(8,128)S(1)} %copy-done.6, f32[8,4,64,2,512,1,1]{4,2,6,1,0,3,5:T(8,128)S(1)} %fusion.20), kind=kOutput, calls=%fused_computation.64 | convolution fusion | flops 12884901888 | bytes 20971520 | tf_op jit(solution)/shard_map/skyrw,rsytq->tqkw/dot_general | solution.py:74
  682.7 10.9 fusion.40
  693.6 16.5 %fusion.80 = f32[4,8,2,4,64,128]{5,4,3,1,0,2:T(8,128)S(1)} fusion(f32[2,512,2,4,128,1,1]{4,1,0,6,5,3,2:T(8,128)} %constant.52, f32[2,8,64,4,512]{4,2,0,3,1:T(8,128)S(1)} %fusion.40), kind=kOutput, calls=%fused_computation.65 | convolution fusion | flops 12884901888 | bytes 20971520 | tf_op jit(solution)/shard_map/srkyw,rwpdx->dspkyx/dot_general | solution.py:74
  710.1 4.2 copy.98
  714.4 9.5 reshape.100
  723.8 73.7 %all-to-all-done.1 = f32[32,8,8192]{2,1,0:T(8,128)} async-done(((f32[32,8,8192]{2,1,0:T(8,128)}), f32[32,8,8192]{2,1,0:T(8,128)}, u32[]{:S(2)}, u32[]{:S(2)}) %all-to-all-start.1) | async-done | bytes 8388640 | tf_op jit(solution)/shard_map/all_to_all | solution.py:71
  797.6 4.2 all-to-all-start.5
  801.7 5.0 copy.131
  806.7 5.0 copy.132
  811.8 17.0 %fusion.26 = f32[8,4,64,2,512,1,1]{4,2,6,1,0,3,5:T(8,128)} fusion(f32[2,4,128,2,512,1,1]{4,2,0,6,5,3,1:T(8,128)} %constant.56, f32[4,8,2,4,64,128,1]{5,4,3,2,1,0,6:T(8,128)S(1)} %bitcast.181), kind=kOutput, calls=%fused_computation.27 | convolution fusion | flops 12884901888 | bytes 20971520 | tf_op jit(solution)/shard_map/dspkyx,pdxrw->skyrw/dot_general | solution.py:74
  828.8 15.7 %fusion.24 = f32[8,4,64,2,512,1,1]{4,2,6,1,0,3,5:T(8,128)} fusion(f32[2,4,128,2,512,1,1]{4,2,0,6,5,3,1:T(8,128)S(1)} %copy-done.9, f32[4,8,2,4,64,128,1]{5,4,3,2,1,0,6:T(8,128)S(1)} %bitcast.178), kind=kOutput, calls=%fused_computation.25 | convolution fusion | flops 12884901888 | bytes 20971520 | tf_op jit(solution)/shard_map/dspkyx,pdxrw->skyrw/dot_general | solution.py:74
  844.5 21.6 %fusion.65 = f32[2,512,4,512]{3,1,2,0:T(8,128)S(1)} fusion(f32[2,8,64,2,512,1]{4,2,1,0,5,3:T(8,128)S(1)} %copy-done.7, f32[8,4,64,2,512,1,1]{4,2,6,1,0,3,5:T(8,128)} %fusion.26), kind=kOutput, calls=%fused_computation.60 | convolution fusion | flops 12884901888 | bytes 20971520 | tf_op jit(solution)/shard_map/skyrw,rsytq->tqkw/dot_general | solution.py:74
  866.1 16.2 %fusion.68 = f32[2,512,4,512]{3,1,2,0:T(8,128)} fusion(f32[2,8,64,2,512,1]{4,2,1,0,5,3:T(8,128)S(1)} %copy-done.7, f32[8,4,64,2,512,1,1]{4,2,6,1,0,3,5:T(8,128)S(1)} %copy-done.10), kind=kOutput, calls=%fused_computation.61 | convolution fusion | flops 12884901888 | bytes 20971520 | tf_op jit(solution)/shard_map/skyrw,rsytq->tqkw/dot_general | solution.py:74
  882.3 10.9 fusion.49
  893.2 16.7 %fusion.71 = f32[4,8,2,4,64,128]{5,4,3,1,0,2:T(8,128)S(1)} fusion(f32[2,512,2,4,128,1,1]{4,1,0,6,5,3,2:T(8,128)} %constant.52, f32[2,8,64,4,512]{4,2,0,3,1:T(8,128)S(1)} %fusion.49), kind=kOutput, calls=%fused_computation.62 | convolution fusion | flops 12884901888 | bytes 20971520 | tf_op jit(solution)/shard_map/srkyw,rwpdx->dspkyx/dot_general | solution.py:74
  909.9 4.2 copy.90
  914.1 9.5 reshape.94
  923.6 62.9 %all-to-all-done.5 = f32[32,8,8192]{2,1,0:T(8,128)} async-done(((f32[32,8,8192]{2,1,0:T(8,128)}), f32[32,8,8192]{2,1,0:T(8,128)}, u32[]{:S(2)}, u32[]{:S(2)}) %all-to-all-start.5) | async-done | bytes 8388640 | tf_op jit(solution)/shard_map/all_to_all | solution.py:71
  990.4 8.3 copy.136
  998.6 176.5 %all-to-all-done.2 = f32[32,8,8192]{2,1,0:T(8,128)} async-done(((f32[32,8,8192]{2,1,0:T(8,128)}), f32[32,8,8192]{2,1,0:T(8,128)}, u32[]{:S(2)}, u32[]{:S(2)}) %all-to-all-start.2) | async-done | bytes 8388640 | tf_op jit(solution)/shard_map/all_to_all | solution.py:71
  1175.1 5.2 copy.133
  1180.3 17.5 %fusion.33 = f32[64,128,512]{2,1,0:T(8,128)} fusion(f32[256,512,1]{1,0,2:T(8,128)S(1)} %copy-done.3, f32[256,64,128]{2,1,0:T(8,128)S(1)} %bitcast.174), kind=kOutput, calls=%fused_computation.34 | convolution fusion | flops 6442450944 | bytes 25690112 | tf_op jit(solution)/shard_map/gyx,gz->xyz/dot_general | solution.py:74
  1197.9 21.4 %add_bitcast_fusion = f32[128,64,512]{2,0,1:T(8,128)} fusion(f32[64,128,512]{2,1,0:T(8,128)} %fusion.33, f32[256,512,1]{1,0,2:T(8,128)S(1)} %copy-done.4, f32[256,64,128]{2,1,0:T(8,128)S(1)} %bitcast.177), kind=kOutput, calls=%fused_computation | convolution fusion | flops 6446645248 | bytes 42467328 | tf_op jit(solution)/shard_map/gyx,gz->xyz/dot_general | solution.py:74
  1219.3 17.8 %copy.100 = f32[128,64,512]{2,1,0:T(8,128)} copy(f32[128,64,512]{2,0,1:T(8,128)} %add_bitcast_fusion) | data formatting | bytes 33554432 | tf_op jit(solution)/shard_map/add | solution.py:100
  (29 shorter events, 4.0 us)
Async XLA Ops:
  39.1 7.6 copy-start.1
  39.1 192.4 %all-to-all-start.3 = ((f32[32,8,8192]{2,1,0:T(8,128)}), f32[32,8,8192]{2,1,0:T(8,128)}, u32[]{:S(2)}, u32[]{:S(2)}) async-start(f32[32,8,8192]{2,1,0:T(8,128)} %reshape.96), calls=%async_computation.3 | async-start | bytes 16777216 | tf_op jit(solution)/shard_map/all_to_all | solution.py:71
  85.8 149.6 %copy-start.2 = (f32[256,512,1]{1,0,2:T(8,128)S(1)}, f32[256,512,1]{1,0,2:T(8,128)}, u32[]{:S(2)}) copy-start(f32[256,512,1]{1,0,2:T(8,128)} %constant.58) | copy-start | bytes 1572868
  231.5 188.7 %all-to-all-start = ((f32[32,8,8192]{2,1,0:T(8,128)}), f32[32,8,8192]{2,1,0:T(8,128)}, u32[]{:S(2)}, u32[]{:S(2)}) async-start(f32[32,8,8192]{2,1,0:T(8,128)} %reshape.90), calls=%async_computation | async-start | bytes 16777216 | tf_op jit(solution)/shard_map/all_to_all | solution.py:71
  420.2 188.9 %all-to-all-start.4 = ((f32[32,8,8192]{2,1,0:T(8,128)}), f32[32,8,8192]{2,1,0:T(8,128)}, u32[]{:S(2)}, u32[]{:S(2)}) async-start(f32[32,8,8192]{2,1,0:T(8,128)} %reshape.98), calls=%async_computation.4 | async-start | bytes 16777216 | tf_op jit(solution)/shard_map/all_to_all | solution.py:71
  463.3 149.6 %copy-start.5 = (pred[512,512]{1,0:T(32,128)(4,1)S(1)}, pred[512,512]{1,0:T(32,128)(4,1)}, u32[]{:S(2)}) copy-start(pred[512,512]{1,0:T(32,128)(4,1)} %constant.39) | copy-start | bytes 786436
  609.1 188.5 %all-to-all-start.1 = ((f32[32,8,8192]{2,1,0:T(8,128)}), f32[32,8,8192]{2,1,0:T(8,128)}, u32[]{:S(2)}, u32[]{:S(2)}) async-start(f32[32,8,8192]{2,1,0:T(8,128)} %reshape.92), calls=%async_computation.1 | async-start | bytes 16777216 | tf_op jit(solution)/shard_map/all_to_all | solution.py:71
  618.1 5.2 copy-start.8
  637.2 14.1 %copy-start.6 = (f32[2,8,64,2,512,1]{4,2,1,0,5,3:T(8,128)S(1)}, f32[2,8,64,2,512,1]{4,2,1,0,5,3:T(8,128)}, u32[]{:S(2)}) copy-start(f32[2,8,64,2,512,1]{4,2,1,0,5,3:T(8,128)} %constant.54) | copy-start | bytes 12582916
  666.5 16.2 %copy-start = (f32[512,2,8,64,1]{0,3,1,4,2:T(8,128)S(1)}, f32[512,2,8,64,1]{0,3,1,4,2:T(8,128)}, u32[]{:S(2)}) copy-start(f32[512,2,8,64,1]{0,3,1,4,2:T(8,128)} %constant.53) | copy-start | bytes 6291460
  797.6 188.9 %all-to-all-start.5 = ((f32[32,8,8192]{2,1,0:T(8,128)}), f32[32,8,8192]{2,1,0:T(8,128)}, u32[]{:S(2)}, u32[]{:S(2)}) async-start(f32[32,8,8192]{2,1,0:T(8,128)} %reshape.100), calls=%async_computation.5 | async-start | bytes 16777216 | tf_op jit(solution)/shard_map/all_to_all | solution.py:71
  811.8 17.0 %copy-start.9 = (f32[2,4,128,2,512,1,1]{4,2,0,6,5,3,1:T(8,128)S(1)}, f32[2,4,128,2,512,1,1]{4,2,0,6,5,3,1:T(8,128)}, u32[]{:S(2)}) copy-start(f32[2,4,128,2,512,1,1]{4,2,0,6,5,3,1:T(8,128)} %constant.56) | copy-start | bytes 12582916
  828.8 15.7 %copy-start.7 = (f32[2,8,64,2,512,1]{4,2,1,0,5,3:T(8,128)S(1)}, f32[2,8,64,2,512,1]{4,2,1,0,5,3:T(8,128)}, u32[]{:S(2)}) copy-start(f32[2,8,64,2,512,1]{4,2,1,0,5,3:T(8,128)} %constant.54) | copy-start | bytes 12582916
  844.5 21.6 %copy-start.10 = (f32[8,4,64,2,512,1,1]{4,2,6,1,0,3,5:T(8,128)S(1)}, f32[8,4,64,2,512,1,1]{4,2,6,1,0,3,5:T(8,128)}, u32[]{:S(2)}) copy-start(f32[8,4,64,2,512,1,1]{4,2,6,1,0,3,5:T(8,128)} %fusion.24) | copy-start | bytes 25165828
  986.5 188.6 %all-to-all-start.2 = ((f32[32,8,8192]{2,1,0:T(8,128)}), f32[32,8,8192]{2,1,0:T(8,128)}, u32[]{:S(2)}, u32[]{:S(2)}) async-start(f32[32,8,8192]{2,1,0:T(8,128)} %reshape.94), calls=%async_computation.2 | async-start | bytes 16777216 | tf_op jit(solution)/shard_map/all_to_all | solution.py:71
  1175.1 5.2 copy-start.3
  1175.1 22.8 %slice-start = ((s8[8388608]{0:T(1024)(128)(4,1)}), s8[4194304]{0:T(1024)(128)(4,1)S(1)}, s32[]{:S(2)}) async-start(s8[8388608]{0:T(1024)(128)(4,1)} %bitcast.175), calls=%async_computation.6 | async-start | bytes 8388608
  1180.3 17.6 %slice-start.1 = ((s8[8388608]{0:T(1024)(128)(4,1)}), s8[4194304]{0:T(1024)(128)(4,1)S(1)}, s32[]{:S(2)}) async-start(s8[8388608]{0:T(1024)(128)(4,1)} %bitcast.175), calls=%async_computation.7 | async-start | bytes 8388608
  1180.3 17.6 %copy-start.4 = (f32[256,512,1]{1,0,2:T(8,128)S(1)}, f32[256,512,1]{1,0,2:T(8,128)}, u32[]{:S(2)}) copy-start(f32[256,512,1]{1,0,2:T(8,128)} %constant.59) | copy-start | bytes 1572868
where the time goes:
time: 1250 us; the launch traced here: 1240 us
  waiting for transfers between devices  750 us (60%)
  matrix products  309 us (25%)
  local copies, waits for them, and re-layouts  150 us (12%)
  starting transfers between devices  27.5 us (2%)
    all_to_all x6, waiting for transfers between devices, exchange(): lax.all_to_all(rows, ('gx', 'gy'), split_axis=0, concat_axis=0, tiled=True)  750 us
    dot_general x18, matrix products, product(): return jnp.einsum(pattern, left, right, precision=split_mode)  309 us
    transpose x6, local copies, waits for them, and re-layouts, product(): return jnp.einsum(pattern, left, right, precision=split_mode)  41.5 us
    reshape x4, local copies, waits for them, and re-layouts, depth_forward(): return exchange(lines.reshape(devices, 2 * per_chunk, y_local * x_local))  37.7 us
    unnamed x33, local copies, waits for them, and re-layouts  33.8 us
    all_to_all x6, starting transfers between devices, exchange(): lax.all_to_all(rows, ('gx', 'gy'), split_axis=0, concat_axis=0, tiled=True)  27.5 us
  transfers between devices with their start and end apart: 6, of which 6 were waited for; matrix products, arithmetic and copies ran while one was open for 29% of the time, Pallas kernels for 0%

commit v1 on v0

v1 whole, which is shorter than its diff:
```python
import functools
import math

import jax
import jax.numpy as jnp
import numpy as np
from jax import lax
from jax.experimental import pallas as pl
from jax.experimental.pallas import tpu as pltpu
from jax.sharding import PartitionSpec as P

MESH = pl.DeviceIdType.MESH
GROUP = 8
LANES = 128
f32 = jnp.float32
bf16 = jnp.bfloat16


def trig(length):
    positions = np.arange(length)
    radians = (positions[:, None] * positions[None, :] % length) * (2.0 * math.pi / length)
    return np.concatenate([np.cos(radians), np.sin(radians)]).astype(np.float32)


def halves(table):
    table = jnp.asarray(table)
    high = table.astype(bf16)
    low = (table - high.astype(f32)).astype(bf16)
    return high, low


def split(values):
    high = values.astype(bf16)
    return high, (values - high.astype(f32)).astype(bf16)


def dot3(left, right, contract):
    def one(a, b):
        return lax.dot_general(a, b, (contract, ((), ())), preferred_element_type=f32)

    (lh, ll), (rh, rl) = left, right
    return one(lh, rh) + one(lh, rl) + one(ll, rh)


def build_rotation(table, out, size, right):
    for part in range(2):
        cos = table[part][0:size, :]
        sin = table[part][size : 2 * size, :]
        out[part][0:size, 0:size] = cos
        out[part][size : 2 * size, size : 2 * size] = cos
        out[part][0:size, size : 2 * size] = -sin if right else sin
        out[part][size : 2 * size, 0:size] = sin if right else -sin


def exchange_kernel(sizes, *refs):
    (count_x, count_y, x_local, y_local, depth, compute) = sizes
    devices = count_x * count_y
    grid_x, grid_y = count_x * x_local, count_y * y_local
    half = depth // 2
    slices = half // devices
    pack = LANES // x_local
    span = GROUP * pack
    groups = y_local // span
    cell_total = float(grid_x * grid_y * depth)
    (d1, d2, xc, xcl, yc_, ycl, zc, zcl,
     back, z1, z2, r1, r2, bs,
     dt, zt, rxh, rxl, ryh, ryl, xh, xl, lh, ll, spec, ph, plo, gh, gl, bt, pf,
     local, sent, got) = refs
    gx, gy = lax.axis_index("gx"), lax.axis_index("gy")
    me = gx * count_y + gy

    def peer(offset):
        dest = lax.rem(me + offset, devices)
        return dest, (dest // count_y, lax.rem(dest, count_y))

    barrier = pltpu.get_barrier_semaphore()

    def greet(offset, _):
        pl.semaphore_signal(barrier, inc=1, device_id=peer(offset)[1], device_id_type=MESH)
        return 0

    lax.fori_loop(1, devices, greet, 0)

    def local_copy(src, dst):
        copy = pltpu.make_async_copy(src, dst, local)
        copy.start()
        copy.wait()

    def send_all(source, target, sem):
        own = pltpu.make_async_copy(source(me), target, got.at[sem])
        own.start()

        def one(offset, _):
            dest, where = peer(offset)
            pltpu.make_async_remote_copy(
                source(dest), target, sent.at[sem], got.at[sem],
                device_id=where, device_id_type=MESH,
            ).start()
            return 0

        lax.fori_loop(1, devices, one, 0)

    def wait_bytes(ref, sem):
        pltpu.make_async_copy(ref, ref, sem).wait()

    rows_all = slices * devices * 2 * GROUP
    depth_tiles = depth // LANES

    def depth_forward(density, z, group):
        for tile in range(depth_tiles):
            pltpu.make_async_copy(
                density.at[:, pl.ds(group * span, span), pl.ds(tile * LANES, LANES)], dt.at[tile], local
            ).start()
        pltpu.make_async_copy(dt, dt, local).wait()
        if compute:
            lines = dt.reshape(depth_tiles * x_local * span, LANES)
            out = zt.reshape(rows_all, LANES)
            for first in range(0, GROUP, 2):
                cells = jnp.concatenate(
                    [
                        jnp.concatenate(
                            [
                                lines[pl.ds(tile * x_local * span + h * GROUP + row, x_local, stride=span), :]
                                for tile in range(depth_tiles)
                            ],
                            axis=1,
                        )
                        for row in (first, first + 1)
                        for h in range(pack)
                    ],
                    axis=0,
                )
                cells = split(cells)
                for c in range(2):
                    table = (zc[c * depth : c * depth + half, :], zcl[c * depth : c * depth + half, :])
                    rows = dot3(table, cells, ((1,), (1,)))
                    if c:
                        rows = -rows
                    for n in range(2):
                        out[pl.ds(c * GROUP + first + n, half, stride=2 * GROUP), :] = rows[
                            :, n * LANES : (n + 1) * LANES
                        ]
        local_copy(zt, z.at[:, :, group])

    def first_field(group, _):
        depth_forward(d1, z1, group)

        @pl.when(group == 0)
        def _():
            pl.semaphore_wait(barrier, devices - 1)

        send_all(lambda dest: z1.at[:, dest, group], r1.at[:, me, group], group)
        return 0

    lax.fori_loop(0, groups, first_field, 0)

    def second_field(group, _):
        depth_forward(d2, z2, group)
        return 0

    lax.fori_loop(0, groups, second_field, 0)
    if compute:
        build_rotation((xc, xcl), (rxh, rxl), grid_x, True)
        build_rotation((yc_, ycl), (ryh, ryl), grid_y, False)

    def unpack_rows(block):
        if pack > 1:
            block = jnp.concatenate(
                [
                    block[..., h * x_local : (h + 1) * x_local].reshape(count_y, groups, 1, GROUP, x_local)
                    for h in range(pack)
                ],
                axis=2,
            )
        return block.reshape(grid_y, x_local)

    def pack_rows(block):
        if pack == 1:
            return block.reshape(count_y, groups, GROUP, x_local)
        block = block.reshape(count_y, groups, pack, GROUP, x_local)
        return jnp.concatenate([block[:, :, h] for h in range(pack)], axis=-1)

    waited = 0
    for k in range(slices):
        upto = (k + 1) * groups // slices
        for group in range(waited, upto):
            wait_bytes(r1.at[:, :, group], got.at[group])
        waited = upto
        send_all(lambda dest: z2.at[k, dest], r2.at[k, me], groups + k)

    tile_x = min(256, grid_x)
    tile_y = min(256, grid_y)
    ky = lax.broadcasted_iota(jnp.int32, (grid_y, grid_x), 0)
    kx = lax.broadcasted_iota(jnp.int32, (grid_y, grid_x), 1)
    keep = (ky != grid_y // 2) & (kx != grid_x // 2)

    def plane(k, _):
        wait_bytes(r2.at[k], got.at[groups + k])
        local_copy(r1.at[k], pf.at[0])
        local_copy(r2.at[k], pf.at[1])
        if compute:
            def forward(field, _):
                cells = pf.at[field].reshape(count_x, count_y, groups, 2, GROUP, LANES)
                for c in range(2):
                    for i in range(count_x):
                        high, low = split(unpack_rows(cells[i, :, :, c]))
                        at = c * grid_x + i * x_local
                        xh[:, at : at + x_local] = high
                        xl[:, at : at + x_local] = low
                for n in range(2 * grid_x // tile_x):
                    cols = slice(n * tile_x, (n + 1) * tile_x)
                    part = dot3((xh[...], xl[...]), (rxh[:, cols], rxl[:, cols]), ((1,), (0,)))
                    c, at = divmod(n * tile_x, grid_x)
                    high, low = split(part)
                    lh[c * grid_y : (c + 1) * grid_y, at : at + tile_x] = high
                    ll[c * grid_y : (c + 1) * grid_y, at : at + tile_x] = low
                for m in range(2 * grid_y // tile_y):
                    rows = slice(m * tile_y, (m + 1) * tile_y)
                    spec[field, rows, :] = dot3((ryh[rows, :], ryl[rows, :]), (lh[...], ll[...]), ((1,), (0,)))
                return 0

            lax.fori_loop(0, 2, forward, 0)
            power = spec[0, 0:grid_y] * spec[1, 0:grid_y] + spec[0, grid_y:] * spec[1, grid_y:]
            weight = jnp.where((k == 0) & (me == 0), 1.0, 2.0).astype(f32) * (1.0 / math.sqrt(cell_total))
            power = jnp.where(keep, power / cell_total, 0.0) * weight
            ph[...], plo[...] = split(power)
            for m in range(2 * grid_y // tile_y):
                rows = slice(m * tile_y, (m + 1) * tile_y)
                part = dot3((yc_[rows, :], ycl[rows, :]), (ph[...], plo[...]), ((1,), (0,)))
                c, at = divmod(m * tile_y, grid_y)
                high, low = split(part)
                gh[at : at + tile_y, c * grid_x : (c + 1) * grid_x] = high
                gl[at : at + tile_y, c * grid_x : (c + 1) * grid_x] = low
            cells = bt.reshape(count_x, count_y, groups, 2, GROUP, LANES)
            for n in range(2 * grid_x // tile_x):
                rows = slice(n * tile_x, (n + 1) * tile_x)
                part = dot3((gh[...], gl[...]), (rxh[rows, :], rxl[rows, :]), ((1,), (1,)))
                c, at = divmod(n * tile_x, grid_x)
                for m in range(tile_x // x_local):
                    i = at // x_local + m
                    cells[i, :, :, c] = pack_rows(part[:, m * x_local : (m + 1) * x_local])
        local_copy(bt, bs.at[k])
        send_all(lambda dest: bs.at[k, dest], back.at[k, me], groups + slices + k)
        return 0

    lax.fori_loop(0, slices, plane, 0)
    for k in range(slices):
        wait_bytes(back.at[k], got.at[groups + slices + k])
    for group in range(groups):
        wait_bytes(z1.at[:, pl.ds(0, devices - 1), group], sent.at[group])
    for k in range(slices):
        wait_bytes(z2.at[k, pl.ds(0, devices - 1)], sent.at[groups + k])
        wait_bytes(bs.at[k, pl.ds(0, devices - 1)], sent.at[groups + slices + k])


def depth_inverse_kernel(x_local, depth, groups, rows_ref, high_ref, low_ref, out_ref, block, done):
    half = depth // 2
    pack = LANES // x_local
    span = GROUP * pack
    depth_tiles = depth // LANES
    rows = rows_ref.reshape(half * 2 * GROUP, LANES)
    group = pl.program_id(0)
    slot = lax.rem(group, 2)

    def finish(slot):
        pltpu.make_async_copy(block.at[slot], block.at[slot], done.at[slot]).wait()

    @pl.when(group >= 2)
    def _():
        finish(slot)

    out = block.at[slot].reshape(depth_tiles * x_local * span, LANES)
    for first in range(0, GROUP, 2):
        total = None
        for c in range(2):
            lines = jnp.concatenate(
                [rows[pl.ds(c * GROUP + first + n, half, stride=2 * GROUP), :] for n in range(2)], axis=1
            )
            table = (
                high_ref[c * depth : c * depth + half, :],
                low_ref[c * depth : c * depth + half, :],
            )
            part = dot3(split(lines), table, ((0,), (0,)))
            total = part if c == 0 else total - part
        for n in range(2):
            for h in range(pack):
                at = n * LANES + h * x_local
                for tile in range(depth_tiles):
                    out[pl.ds(tile * x_local * span + h * GROUP + first + n, x_local, stride=span), :] = total[
                        at : at + x_local, tile * LANES : (tile + 1) * LANES
                    ]
    for tile in range(depth_tiles):
        pltpu.make_async_copy(
            block.at[slot, tile],
            out_ref.at[:, pl.ds(group * span, span), pl.ds(tile * LANES, LANES)],
            done.at[slot],
        ).start()

    @pl.when(group == groups - 1)
    def _():
        for other in range(min(2, groups)):
            finish(other)


def on_device(compute, density_one, density_two):
    count_x = lax.axis_size("gx")
    count_y = lax.axis_size("gy")
    devices = count_x * count_y
    x_local, y_local, depth = density_one.shape
    grid_x, grid_y = x_local * count_x, y_local * count_y
    slices = depth // 2 // devices
    span = GROUP * (LANES // x_local)
    groups = y_local // span
    tables = {length: halves(trig(length)) for length in {grid_x, grid_y, depth}}
    packed = jax.ShapeDtypeStruct((slices, devices, groups, 2 * GROUP, LANES), f32)
    vmem = pl.BlockSpec(memory_space=pltpu.VMEM)
    hbm = pl.BlockSpec(memory_space=pl.ANY)
    scratch = [
        pltpu.VMEM((depth // LANES, x_local, span, LANES), f32),
        pltpu.VMEM((slices, devices, 2 * GROUP, LANES), f32),
        pltpu.VMEM((2 * grid_x, 2 * grid_x), bf16),
        pltpu.VMEM((2 * grid_x, 2 * grid_x), bf16),
        pltpu.VMEM((2 * grid_y, 2 * grid_y), bf16),
        pltpu.VMEM((2 * grid_y, 2 * grid_y), bf16),
        pltpu.VMEM((grid_y, 2 * grid_x), bf16),
        pltpu.VMEM((grid_y, 2 * grid_x), bf16),
        pltpu.VMEM((2 * grid_y, grid_x), bf16),
        pltpu.VMEM((2 * grid_y, grid_x), bf16),
        pltpu.VMEM((2, 2 * grid_y, grid_x), f32),
        pltpu.VMEM((grid_y, grid_x), bf16),
        pltpu.VMEM((grid_y, grid_x), bf16),
        pltpu.VMEM((grid_y, 2 * grid_x), bf16),
        pltpu.VMEM((grid_y, 2 * grid_x), bf16),
        pltpu.VMEM((devices, groups, 2 * GROUP, LANES), f32),
        pltpu.VMEM((2, devices, groups, 2 * GROUP, LANES), f32),
        pltpu.SemaphoreType.DMA,
        pltpu.SemaphoreType.DMA((groups + 2 * slices,)),
        pltpu.SemaphoreType.DMA((groups + 2 * slices,)),
    ]
    sizes = (count_x, count_y, x_local, y_local, depth, compute)
    back = pl.pallas_call(
        functools.partial(exchange_kernel, sizes),
        out_shape=[packed] * 6,
        in_specs=[hbm] * 2 + [vmem] * 6,
        out_specs=[hbm] * 6,
        scratch_shapes=scratch,
        compiler_params=pltpu.CompilerParams(
            collective_id=0, has_side_effects=True, vmem_limit_bytes=60 * 2**20
        ),
    )(density_one, density_two, *tables[grid_x], *tables[grid_y], *tables[depth])[0]
    return pl.pallas_call(
        functools.partial(depth_inverse_kernel, x_local, depth, groups),
        grid=(groups,),
        out_shape=jax.ShapeDtypeStruct(density_one.shape, f32),
        in_specs=[
            pl.BlockSpec((slices, devices, 1, 2 * GROUP, LANES), lambda g: (0, 0, g, 0, 0)),
            pl.BlockSpec((2 * depth, depth), lambda g: (0, 0)),
            pl.BlockSpec((2 * depth, depth), lambda g: (0, 0)),
        ],
        out_specs=hbm,
        scratch_shapes=[
            pltpu.VMEM((2, depth // LANES, x_local, span, LANES), f32),
            pltpu.SemaphoreType.DMA((2,)),
        ],
        compiler_params=pltpu.CompilerParams(vmem_limit_bytes=48 * 2**20),
    )(back, *tables[depth])


def solution(mesh, compute=True):
    return jax.shard_map(
        functools.partial(on_device, compute),
        mesh=mesh,
        in_specs=(P("gx", "gy", None), P("gx", "gy", None)),
        out_specs=P("gx", "gy", None),
        check_vma=False,
    )
```

time: 1250 us -> 1130 us (0.904)
  Pallas kernels: 0 us -> 1120 us
  waiting for transfers between devices: 750 us -> 0 us
  matrix products: 309 us -> 0 us
  local copies, waits for them, and re-layouts: 150 us -> 0.01 us
  starting transfers between devices: 27.5 us -> 0 us
    pallas_call x0 -> x2, Pallas kernels: none -> 1120 us  [the longest x1 1100 us: on_device(): pl.pallas_call(functools.partial(exchange_kernel, sizes), out_shape=[pack...]
    all_to_all x6 -> x0, waiting for transfers between devices: 750 us -> none  [exchange(): lax.all_to_all(rows, ('gx', 'gy'), split_axis=0, concat_axis=0, tiled=True)]
    dot_general x18 -> x0, matrix products: 309 us -> none  [product(): return jnp.einsum(pattern, left, right, precision=split_mode)]
    reshape x6 -> x0, local copies, waits for them, and re-layouts: 56.7 us -> none  [the longest x4 37.7 us: depth_forward(): return exchange(lines.reshape(devices, 2 * per_chunk, y_local * x_local))]
    transpose x6 -> x0, local copies, waits for them, and re-layouts: 41.5 us -> none  [product(): return jnp.einsum(pattern, left, right, precision=split_mode)]
    unnamed x33 -> x4, local copies, waits for them, and re-layouts: 33.8 us -> 0.01 us
    all_to_all x6 -> x0, starting transfers between devices: 27.5 us -> none  [exchange(): lax.all_to_all(rows, ('gx', 'gy'), split_axis=0, concat_axis=0, tiled=True)]
    add x1 -> x0, local copies, waits for them, and re-layouts: 17.8 us -> none  [on_device(): correlation = part if correlation is None else correlation + part]
  transfers between devices with their start and end apart: 6 -> 0, of which waited for: 6 -> 0; matrix products, arithmetic and copies ran while one was open for 29% -> 0% of each run, Pallas kernels for 0% -> 0%
where the time goes in v1:
time: 1130 us; the launch traced here: 1120 us
  Pallas kernels  1120 us (99%)
    pallas_call x1, Pallas kernels, on_device(): pl.pallas_call(functools.partial(exchange_kernel, sizes), out_shape=[pack...  1100 us
    pallas_call x1, Pallas kernels, on_device(): pl.pallas_call(functools.partial(depth_inverse_kernel, x_local, depth, gr...  24.9 us

profile of v1, /device:TPU:0, one launch (start us, length us, event | category | flops | bytes accessed | tf_op | source)
XLA Modules:
  0.0 1124.2 jit_solution(1379863503937267647)
XLA Ops:
  0.0 0.0 copy-start
  0.0 0.0 copy-start.1
  0.0 1099.1 %shard_map.37 = (f32[8,32,8,16,128]{4,3,2,1,0:T(8,128)}, f32[8,32,8,16,128]{4,3,2,1,0:T(8,128)}, f32[8,32,8,16,128]{4,3,2,1,0:T(8,128)}, f32[8,32,8,16,128]{4,3,...) custom-call(f32[128,64,512]{2,1,0:T(8,128)} %refs_0_.1, f32[128,64,512]{2,1,0:T(8,128)} %refs_1_.1, ...), custom_call_target="tpu_custom_call" | custom-call | tf_op jit(solution)/shard_map/pallas_call | solution.py:341
  1099.1 0.0 copy-done
  1099.1 0.0 copy-done.1
  1099.2 24.9 %shard_map.38 = f32[128,64,512]{2,1,0:T(8,128)} custom-call(f32[8,32,8,16,128]{4,3,2,1,0:T(8,128)} %get-tuple-element.6.rows_ref, bf16[1024,512]{1,0:T(8,128)(2,1)S(1)} %copy-done.1, bf16[1024,512]{1,0:T(8,128)(2,1)S(1)} %copy-done), custom_call_target="tpu_custom_call" | custom-call | tf_op jit(solution)/shard_map/pallas_call | solution.py:351
Async XLA Ops:
  0.0 1099.1 %copy-start = (bf16[1024,512]{1,0:T(8,128)(2,1)S(1)}, bf16[1024,512]{1,0:T(8,128)(2,1)}, u32[]{:S(2)}) copy-start(bf16[1024,512]{1,0:T(8,128)(2,1)} %constant.6.refs_3_.refs_5_.refs_7_.low_ref) | copy-start | bytes 3145732
  0.0 1099.1 %copy-start.1 = (bf16[1024,512]{1,0:T(8,128)(2,1)S(1)}, bf16[1024,512]{1,0:T(8,128)(2,1)}, u32[]{:S(2)}) copy-start(bf16[1024,512]{1,0:T(8,128)(2,1)} %constant.3.refs_2_.refs_4_.refs_6_.high_ref) | copy-start | bytes 3145732

commit v2 on v1

v2 whole, which is shorter than its diff:
```python
import functools
import math

import jax
import jax.numpy as jnp
import numpy as np
from jax import lax
from jax.experimental import pallas as pl
from jax.experimental.pallas import tpu as pltpu
from jax.sharding import PartitionSpec as P

MESH = pl.DeviceIdType.MESH
GROUP = 8
LANES = 128
f32 = jnp.float32
bf16 = jnp.bfloat16


def trig(length):
    positions = np.arange(length)
    radians = (positions[:, None] * positions[None, :] % length) * (2.0 * math.pi / length)
    return np.concatenate([np.cos(radians), np.sin(radians)]).astype(np.float32)


def halves(table):
    table = jnp.asarray(table)
    high = table.astype(bf16)
    low = (table - high.astype(f32)).astype(bf16)
    return high, low


def split(values):
    high = values.astype(bf16)
    return high, (values - high.astype(f32)).astype(bf16)


def dot3(left, right, contract):
    def one(a, b):
        return lax.dot_general(a, b, (contract, ((), ())), preferred_element_type=f32)

    (lh, ll), (rh, rl) = left, right
    return one(lh, rh) + one(lh, rl) + one(ll, rh)


def build_rotation(table, out, size, right):
    for part in range(2):
        cos = table[part][0:size, :]
        sin = table[part][size : 2 * size, :]
        out[part][0:size, 0:size] = cos
        out[part][size : 2 * size, size : 2 * size] = cos
        out[part][0:size, size : 2 * size] = -sin if right else sin
        out[part][size : 2 * size, 0:size] = sin if right else -sin


def interleave(lines, count, x_local, span, out):
    for row in range(GROUP):
        cells = jnp.concatenate(
            [lines[pl.ds(c * GROUP + row, count, stride=2 * GROUP), :] for c in range(2)], axis=0
        ).T
        for h in range(span // GROUP):
            for tile in range(2 * count // LANES):
                out[pl.ds(tile * x_local * span + h * GROUP + row, x_local, stride=span), :] = cells[
                    h * x_local : (h + 1) * x_local, tile * LANES : (tile + 1) * LANES
                ]


def interleaved_rows(lines, rows):
    return split(jnp.concatenate([lines[tile, rows, :] for tile in range(lines.shape[0])], axis=1))


def tail_slices(slices):
    return max(1, slices // 4)


def exchange_kernel(sizes, *refs):
    count_x, count_y, x_local, y_local, depth = sizes
    devices = count_x * count_y
    grid_x, grid_y = count_x * x_local, count_y * y_local
    half = depth // 2
    slices = half // devices
    pack = LANES // x_local
    span = GROUP * pack
    groups = y_local // span
    cell_total = float(grid_x * grid_y * depth)
    lengths = sorted({grid_x, grid_y, depth})
    d1, d2, *refs = refs
    tables = {length: (refs[2 * n], refs[2 * n + 1]) for n, length in enumerate(lengths)}
    (back, partial, z1, z2, r1, r2, bs,
     dt, zt, rxh, rxl, ryh, ryl, xh, xl, lh, ll, spec, ph, plo, gh, gl, bt, pf, early_rows, early_table, turned, block,
     local, sent, got) = refs[2 * len(lengths) :]
    (yc_, ycl), (zc, zcl) = tables[grid_y], tables[depth]
    gx, gy = lax.axis_index("gx"), lax.axis_index("gy")
    me = gx * count_y + gy

    def peer(offset):
        dest = lax.rem(me + offset, devices)
        return dest, (dest // count_y, lax.rem(dest, count_y))

    barrier = pltpu.get_barrier_semaphore()

    def greet(offset, _):
        pl.semaphore_signal(barrier, inc=1, device_id=peer(offset)[1], device_id_type=MESH)
        return 0

    lax.fori_loop(1, devices, greet, 0)

    def local_copy(src, dst):
        copy = pltpu.make_async_copy(src, dst, local)
        copy.start()
        copy.wait()

    def send_all(source, target, sem):
        own = pltpu.make_async_copy(source(me), target, got.at[sem])
        own.start()

        def one(offset, _):
            dest, where = peer(offset)
            pltpu.make_async_remote_copy(
                source(dest), target, sent.at[sem], got.at[sem],
                device_id=where, device_id_type=MESH,
            ).start()
            return 0

        lax.fori_loop(1, devices, one, 0)

    def wait_bytes(ref, sem):
        pltpu.make_async_copy(ref, ref, sem).wait()

    rows_all = slices * devices * 2 * GROUP
    depth_tiles = depth // LANES

    def load_cells(density, group):
        for tile in range(depth_tiles):
            pltpu.make_async_copy(
                density.at[:, pl.ds(group * span, span), pl.ds(tile * LANES, LANES)], dt.at[tile], local
            ).start()
        pltpu.make_async_copy(dt, dt, local).wait()

    lines = dt.reshape(depth_tiles * x_local * span, LANES)
    packed_rows = zt.reshape(2 * rows_all, LANES)

    def forward_group(step, _):
        group = lax.rem(step, groups)

        @pl.when(step < groups)
        def _():
            load_cells(d1, group)

        @pl.when(step >= groups)
        def _():
            load_cells(d2, group)

        slot = jnp.minimum(step, 1)
        for first in range(0, GROUP, 2):
            cells = jnp.concatenate(
                [
                    jnp.concatenate(
                        [
                            lines[pl.ds(tile * x_local * span + h * GROUP + row, x_local, stride=span), :]
                            for tile in range(depth_tiles)
                        ],
                        axis=1,
                    )
                    for row in (first, first + 1)
                    for h in range(pack)
                ],
                axis=0,
            )
            cells = split(cells)
            for c in range(2):
                table = (zc[c * depth : c * depth + half, :], zcl[c * depth : c * depth + half, :])
                rows = dot3(table, cells, ((1,), (1,)))
                if c:
                    rows = -rows
                for n in range(2):
                    packed_rows[
                        pl.ds(slot * rows_all + c * GROUP + first + n, half, stride=2 * GROUP), :
                    ] = rows[:, n * LANES : (n + 1) * LANES]

        @pl.when(step == 0)
        def _():
            pl.semaphore_wait(barrier, devices - 1)
            send_all(lambda dest: zt.at[0, :, dest], r1.at[:, me, 0], 0)

        @pl.when((step > 0) & (step < groups))
        def _():
            local_copy(zt.at[1], z1.at[:, :, group])
            send_all(lambda dest: z1.at[:, dest, group], r1.at[:, me, group], group)

        @pl.when(step >= groups)
        def _():
            local_copy(zt.at[1], z2.at[:, :, group])

        return 0

    lax.fori_loop(0, 2 * groups, forward_group, 0)
    build_rotation(tables[grid_x], (rxh, rxl), grid_x, True)
    build_rotation(tables[grid_y], (ryh, ryl), grid_y, False)

    def unpack_rows(block):
        if pack > 1:
            block = jnp.concatenate(
                [
                    block[..., h * x_local : (h + 1) * x_local].reshape(count_y, groups, 1, GROUP, x_local)
                    for h in range(pack)
                ],
                axis=2,
            )
        return block.reshape(grid_y, x_local)

    def pack_rows(block):
        if pack == 1:
            return block.reshape(count_y, groups, GROUP, x_local)
        block = block.reshape(count_y, groups, pack, GROUP, x_local)
        return jnp.concatenate([block[:, :, h] for h in range(pack)], axis=-1)

    waited = 0
    for k in range(slices):
        upto = (k + 1) * groups // slices
        for group in range(waited, upto):
            wait_bytes(r1.at[:, :, group], got.at[group])
        waited = upto
        send_all(lambda dest: z2.at[k, dest], r2.at[k, me], groups + k)

    tile_x = min(256, grid_x)
    tile_y = min(256, grid_y)
    ky = lax.broadcasted_iota(jnp.int32, (grid_y, grid_x), 0)
    kx = lax.broadcasted_iota(jnp.int32, (grid_y, grid_x), 1)
    keep = (ky != grid_y // 2) & (kx != grid_x // 2)

    def plane(k, _):
        wait_bytes(r2.at[k], got.at[groups + k])
        local_copy(r1.at[k], pf.at[0])
        local_copy(r2.at[k], pf.at[1])
        def forward(field, _):
            cells = pf.at[field].reshape(count_x, count_y, groups, 2, GROUP, LANES)
            for c in range(2):
                for i in range(count_x):
                    high, low = split(unpack_rows(cells[i, :, :, c]))
                    at = c * grid_x + i * x_local
                    xh[:, at : at + x_local] = high
                    xl[:, at : at + x_local] = low
            for n in range(2 * grid_x // tile_x):
                cols = slice(n * tile_x, (n + 1) * tile_x)
                part = dot3((xh[...], xl[...]), (rxh[:, cols], rxl[:, cols]), ((1,), (0,)))
                c, at = divmod(n * tile_x, grid_x)
                high, low = split(part)
                lh[c * grid_y : (c + 1) * grid_y, at : at + tile_x] = high
                ll[c * grid_y : (c + 1) * grid_y, at : at + tile_x] = low
            for m in range(2 * grid_y // tile_y):
                rows = slice(m * tile_y, (m + 1) * tile_y)
                spec[field, rows, :] = dot3((ryh[rows, :], ryl[rows, :]), (lh[...], ll[...]), ((1,), (0,)))
            return 0

        lax.fori_loop(0, 2, forward, 0)
        power = spec[0, 0:grid_y] * spec[1, 0:grid_y] + spec[0, grid_y:] * spec[1, grid_y:]
        weight = jnp.where((k == 0) & (me == 0), 1.0, 2.0).astype(f32) * (1.0 / math.sqrt(cell_total))
        power = jnp.where(keep, power / cell_total, 0.0) * weight
        ph[...], plo[...] = split(power)
        for m in range(2 * grid_y // tile_y):
            rows = slice(m * tile_y, (m + 1) * tile_y)
            part = dot3((yc_[rows, :], ycl[rows, :]), (ph[...], plo[...]), ((1,), (0,)))
            c, at = divmod(m * tile_y, grid_y)
            high, low = split(part)
            gh[at : at + tile_y, c * grid_x : (c + 1) * grid_x] = high
            gl[at : at + tile_y, c * grid_x : (c + 1) * grid_x] = low
        cells = bt.reshape(count_x, count_y, groups, 2, GROUP, LANES)
        for n in range(2 * grid_x // tile_x):
            rows = slice(n * tile_x, (n + 1) * tile_x)
            part = dot3((gh[...], gl[...]), (rxh[rows, :], rxl[rows, :]), ((1,), (1,)))
            c, at = divmod(n * tile_x, grid_x)
            for m in range(tile_x // x_local):
                i = at // x_local + m
                cells[i, :, :, c] = pack_rows(part[:, m * x_local : (m + 1) * x_local])
        local_copy(bt, bs.at[k])
        send_all(lambda dest: bs.at[k, dest], back.at[k, me], groups + slices + k)
        return 0

    lax.fori_loop(0, slices, plane, 0)
    tail = tail_slices(slices)
    early = slices - tail
    for k in range(early):
        wait_bytes(back.at[k], got.at[groups + slices + k])
    if early:
        count = early * devices
        for part in range(2):
            table = tables[depth][part]
            early_table[part, 0:count, :] = table[0:count, :]
            early_table[part, count : 2 * count, :] = -table[depth : depth + count, :]
        early_lines = early_rows.reshape(count * 2 * GROUP, LANES)
        early_out = turned.reshape(2 * count // LANES * x_local * span, LANES)
        block_rows = block.reshape(x_local * span, depth)
        height = min(256, x_local * span)

        def early_group(group, _):
            local_copy(back.at[pl.ds(0, early), :, group], early_rows)
            interleave(early_lines, count, x_local, span, early_out)

            def strip(m, _):
                rows = pl.ds(pl.multiple_of(m * height, height), height)
                block_rows[rows, :] = dot3(
                    interleaved_rows(turned, rows), (early_table[0], early_table[1]), ((1,), (0,))
                )
                return 0

            lax.fori_loop(0, x_local * span // height, strip, 0)
            local_copy(block, partial.at[:, pl.ds(pl.multiple_of(group * span, span), span), :])
            return 0

        lax.fori_loop(0, groups, early_group, 0)
    for k in range(early, slices):
        wait_bytes(back.at[k], got.at[groups + slices + k])
    wait_bytes(zt.at[0, :, pl.ds(0, devices - 1)], sent.at[0])
    for group in range(1, groups):
        wait_bytes(z1.at[:, pl.ds(0, devices - 1), group], sent.at[group])
    for k in range(slices):
        wait_bytes(z2.at[k, pl.ds(0, devices - 1)], sent.at[groups + k])
        wait_bytes(bs.at[k, pl.ds(0, devices - 1)], sent.at[groups + slices + k])


def depth_inverse_kernel(has_partial, rows_ref, ch, cl, sh, sl, partial_ref, out_ref, turned, table):
    x_local, span, depth = out_ref.shape
    tail, devices = rows_ref.shape[:2]
    count = tail * devices
    lines = rows_ref.reshape(count * 2 * GROUP, LANES)

    @pl.when(pl.program_id(0) == 0)
    def _():
        for n, part in enumerate((ch[...], -sh[...], cl[...], -sl[...], ch[...], -sh[...])):
            table[n * count : (n + 1) * count, :] = part

    interleave(lines, count, x_local, span, turned.reshape(turned.shape[0] * x_local * span, LANES))
    out = out_ref.reshape(x_local * span, depth)
    partial = partial_ref.reshape(x_local * span, depth)
    height = min(512, x_local * span)
    for m in range(x_local * span // height):
        rows = slice(m * height, (m + 1) * height)
        high, low = interleaved_rows(turned, rows)
        total = lax.dot_general(
            jnp.concatenate([high, high, low], axis=1), table[...], (((1,), (0,)), ((), ())), preferred_element_type=f32
        )
        out[rows, :] = total + partial[rows, :] if has_partial else total


def on_device(density_one, density_two):
    count_x = lax.axis_size("gx")
    count_y = lax.axis_size("gy")
    devices = count_x * count_y
    x_local, y_local, depth = density_one.shape
    grid_x, grid_y = x_local * count_x, y_local * count_y
    slices = depth // 2 // devices
    span = GROUP * (LANES // x_local)
    groups = y_local // span
    tail = tail_slices(slices)
    early = slices - tail
    lengths = sorted({grid_x, grid_y, depth})
    tables = {length: halves(trig(length)) for length in lengths}
    packed = jax.ShapeDtypeStruct((slices, devices, groups, 2 * GROUP, LANES), f32)
    vmem = pl.BlockSpec(memory_space=pltpu.VMEM)
    hbm = pl.BlockSpec(memory_space=pl.ANY)
    scratch = [
        pltpu.VMEM((depth // LANES, x_local, span, LANES), f32),
        pltpu.VMEM((2, slices, devices, 2 * GROUP, LANES), f32),
        pltpu.VMEM((2 * grid_x, 2 * grid_x), bf16),
        pltpu.VMEM((2 * grid_x, 2 * grid_x), bf16),
        pltpu.VMEM((2 * grid_y, 2 * grid_y), bf16),
        pltpu.VMEM((2 * grid_y, 2 * grid_y), bf16),
        pltpu.VMEM((grid_y, 2 * grid_x), bf16),
        pltpu.VMEM((grid_y, 2 * grid_x), bf16),
        pltpu.VMEM((2 * grid_y, grid_x), bf16),
        pltpu.VMEM((2 * grid_y, grid_x), bf16),
        pltpu.VMEM((2, 2 * grid_y, grid_x), f32),
        pltpu.VMEM((grid_y, grid_x), bf16),
        pltpu.VMEM((grid_y, grid_x), bf16),
        pltpu.VMEM((grid_y, 2 * grid_x), bf16),
        pltpu.VMEM((grid_y, 2 * grid_x), bf16),
        pltpu.VMEM((devices, groups, 2 * GROUP, LANES), f32),
        pltpu.VMEM((2, devices, groups, 2 * GROUP, LANES), f32),
        pltpu.VMEM((max(1, early), devices, 2 * GROUP, LANES), f32),
        pltpu.VMEM((2, max(1, early) * devices * 2, depth), bf16),
        pltpu.VMEM((max(1, early) * devices * 2 // LANES, x_local * span, LANES), f32),
        pltpu.VMEM((x_local, span, depth), f32),
        pltpu.SemaphoreType.DMA,
        pltpu.SemaphoreType.DMA((groups + 2 * slices,)),
        pltpu.SemaphoreType.DMA((groups + 2 * slices,)),
    ]
    sizes = (count_x, count_y, x_local, y_local, depth)
    back, partial = pl.pallas_call(
        functools.partial(exchange_kernel, sizes),
        out_shape=[packed, jax.ShapeDtypeStruct(density_one.shape, f32)] + [packed] * 5,
        in_specs=[hbm] * 2 + [vmem] * (2 * len(lengths)),
        out_specs=[hbm] * 7,
        scratch_shapes=scratch,
        compiler_params=pltpu.CompilerParams(
            collective_id=0, has_side_effects=True, vmem_limit_bytes=60 * 2**20
        ),
    )(density_one, density_two, *(part for length in lengths for part in tables[length]))[:2]
    count = tail * devices
    cosines = pl.BlockSpec((count, depth), lambda g: (early // tail, 0))
    sines = pl.BlockSpec((count, depth), lambda g: (depth // count + early // tail, 0))
    high, low = tables[depth]
    block = pl.BlockSpec((x_local, span, depth), lambda g: (0, g, 0))
    return pl.pallas_call(
        functools.partial(depth_inverse_kernel, early > 0),
        grid=(groups,),
        out_shape=jax.ShapeDtypeStruct(density_one.shape, f32),
        in_specs=[
            pl.BlockSpec((tail, devices, 1, 2 * GROUP, LANES), lambda g: (early // tail, 0, g, 0, 0)),
            cosines,
            cosines,
            sines,
            sines,
            block,
        ],
        out_specs=block,
        scratch_shapes=[
            pltpu.VMEM((2 * count // LANES, x_local * span, LANES), f32),
            pltpu.VMEM((6 * count, depth), bf16),
        ],
        compiler_params=pltpu.CompilerParams(vmem_limit_bytes=48 * 2**20),
    )(back, high, low, high, low, partial)


def solution(mesh):
    return jax.shard_map(
        on_device,
        mesh=mesh,
        in_specs=(P("gx", "gy", None), P("gx", "gy", None)),
        out_specs=P("gx", "gy", None),
        check_vma=False,
    )
```

time: 1130 us -> 1120 us (level)
  no operation moved by 1% of the time
where the time goes in v2:
time: 1120 us
  Pallas kernels  1120 us (100%)
    pallas_call x1, Pallas kernels, on_device(): pl.pallas_call(functools.partial(exchange_kernel, sizes), out_shape=[pack...  1100 us

profile of v2, /device:TPU:0, one launch (start us, length us, event | category | flops | bytes accessed | tf_op | source)
XLA Modules:
  0.0 1115.7 jit_solution(16258166530320353751)
XLA Ops:
  0.0 0.0 copy-start
  0.0 0.0 copy-start.1
  0.0 1098.1 %shard_map.37 = (f32[8,32,8,16,128]{4,3,2,1,0:T(8,128)}, f32[128,64,512]{2,1,0:T(8,128)}, f32[8,32,8,16,128]{4,3,2,1,0:T(8,128)}, f32[8,32,8,16,128]{4,3,2,1,0:T...) custom-call(f32[128,64,512]{2,1,0:T(8,128)} %refs_0_.1, ...), custom_call_target="tpu_custom_call" | custom-call | tf_op jit(solution)/shard_map/pallas_call | solution.py:388
  1098.1 0.0 copy-done
  1098.1 0.0 copy-done.1
  1098.1 17.6 %shard_map.38 = f32[128,64,512]{2,1,0:T(8,128)} custom-call(f32[8,32,8,16,128]{4,3,2,1,0:T(8,128)} %get-tuple-element.7.rows_ref, bf16[1024,512]{1,0:T(8,128)(2,1)S(1)} %copy-done.1, bf16[1024,512]{1,0:T(8,128)(2,1)S(1)} %copy-done, bf16[1024,512]{1,0:T(8,128)(2,1)S(1)} %copy-done.1, bf16[1024,512]{1,0:T(8,128)(2,1)S(1)} %copy-done, ...), custom_call_target="tpu_custom_call" | custom-call | tf_op jit(solution)/shard_map/pallas_call | solution.py:403
Async XLA Ops:
  0.0 1098.1 %copy-start = (bf16[1024,512]{1,0:T(8,128)(2,1)S(1)}, bf16[1024,512]{1,0:T(8,128)(2,1)}, u32[]{:S(2)}) copy-start(bf16[1024,512]{1,0:T(8,128)(2,1)} %constant.6.refs_3_.cl.sl) | copy-start | bytes 3145732
  0.0 1098.1 %copy-start.1 = (bf16[1024,512]{1,0:T(8,128)(2,1)S(1)}, bf16[1024,512]{1,0:T(8,128)(2,1)}, u32[]{:S(2)}) copy-start(bf16[1024,512]{1,0:T(8,128)(2,1)} %constant.3.refs_2_.ch.sh) | copy-start | bytes 3145732

commit v3 on v2

--- a/solution.py
+++ b/solution.py
@@ -52,10 +52,10 @@
         out[part][size : 2 * size, 0:size] = sin if right else -sin
 
 
-def interleave(lines, count, x_local, span, out):
+def interleave(lines, count, x_local, span, out, base=0):
     for row in range(GROUP):
         cells = jnp.concatenate(
-            [lines[pl.ds(c * GROUP + row, count, stride=2 * GROUP), :] for c in range(2)], axis=0
+            [lines[pl.ds(base + c * GROUP + row, count, stride=2 * GROUP), :] for c in range(2)], axis=0
         ).T
         for h in range(span // GROUP):
             for tile in range(2 * count // LANES):
@@ -87,7 +87,7 @@
     tables = {length: (refs[2 * n], refs[2 * n + 1]) for n, length in enumerate(lengths)}
     (back, partial, z1, z2, r1, r2, bs,
      dt, zt, rxh, rxl, ryh, ryl, xh, xl, lh, ll, spec, ph, plo, gh, gl, bt, pf, early_rows, early_table, turned, block,
-     local, sent, got) = refs[2 * len(lengths) :]
+     local, sent, got, fetched, written) = refs[2 * len(lengths) :]
     (yc_, ycl), (zc, zcl) = tables[grid_y], tables[depth]
     gx, gy = lax.axis_index("gx"), lax.axis_index("gy")
     me = gx * count_y + gy
@@ -287,27 +287,56 @@
             table = tables[depth][part]
             early_table[part, 0:count, :] = table[0:count, :]
             early_table[part, count : 2 * count, :] = -table[depth : depth + count, :]
-        early_lines = early_rows.reshape(count * 2 * GROUP, LANES)
-        early_out = turned.reshape(2 * count // LANES * x_local * span, LANES)
-        block_rows = block.reshape(x_local * span, depth)
-        height = min(256, x_local * span)
+        row_count = count * 2 * GROUP
+        cell_count = x_local * span
+        early_lines = early_rows.reshape(2 * row_count, LANES)
+        early_out = turned.reshape(2 * count // LANES * cell_count, LANES)
+        block_rows = block.reshape(2 * cell_count, depth)
+        height = min(256, cell_count)
+
+        def fetch(group, slot):
+            return pltpu.make_async_copy(
+                back.at[pl.ds(0, early), :, group], early_rows.at[slot], fetched.at[slot]
+            )
+
+        def stored(slot):
+            pltpu.make_async_copy(block.at[slot], block.at[slot], written.at[slot]).wait()
+
+        fetch(0, 0).start()
 
         def early_group(group, _):
-            local_copy(back.at[pl.ds(0, early), :, group], early_rows)
-            interleave(early_lines, count, x_local, span, early_out)
+            slot = lax.rem(group, 2)
+            fetch(group, slot).wait()
+
+            @pl.when(group < groups - 1)
+            def _():
+                fetch(group + 1, 1 - slot).start()
+
+            @pl.when(group >= 2)
+            def _():
+                stored(slot)
+
+            interleave(early_lines, count, x_local, span, early_out, slot * row_count)
 
             def strip(m, _):
                 rows = pl.ds(pl.multiple_of(m * height, height), height)
-                block_rows[rows, :] = dot3(
+                target = pl.ds(pl.multiple_of(slot * cell_count + m * height, height), height)
+                block_rows[target, :] = dot3(
                     interleaved_rows(turned, rows), (early_table[0], early_table[1]), ((1,), (0,))
                 )
                 return 0
 
-            lax.fori_loop(0, x_local * span // height, strip, 0)
-            local_copy(block, partial.at[:, pl.ds(pl.multiple_of(group * span, span), span), :])
+            lax.fori_loop(0, cell_count // height, strip, 0)
+            pltpu.make_async_copy(
+                block.at[slot],
+                partial.at[:, pl.ds(pl.multiple_of(group * span, span), span), :],
+                written.at[slot],
+            ).start()
             return 0
 
         lax.fori_loop(0, groups, early_group, 0)
+        for slot in range(min(2, groups)):
+            stored(slot)
     for k in range(early, slices):
         wait_bytes(back.at[k], got.at[groups + slices + k])
     wait_bytes(zt.at[0, :, pl.ds(0, devices - 1)], sent.at[0])
@@ -318,28 +347,63 @@
         wait_bytes(bs.at[k, pl.ds(0, devices - 1)], sent.at[groups + slices + k])
 
 
-def depth_inverse_kernel(has_partial, rows_ref, ch, cl, sh, sl, partial_ref, out_ref, turned, table):
-    x_local, span, depth = out_ref.shape
-    tail, devices = rows_ref.shape[:2]
+def depth_inverse_kernel(
+    early, back, high, low, partial, out, lines, cells, turned, parts, table, tables_in, lines_in, cells_in, cells_out
+):
+    groups, x_local, span, depth = cells.shape
+    tail, devices = lines.shape[1:3]
     count = tail * devices
-    lines = rows_ref.reshape(count * 2 * GROUP, LANES)
-
-    @pl.when(pl.program_id(0) == 0)
-    def _():
-        for n, part in enumerate((ch[...], -sh[...], cl[...], -sl[...], ch[...], -sh[...])):
-            table[n * count : (n + 1) * count, :] = part
-
-    interleave(lines, count, x_local, span, turned.reshape(turned.shape[0] * x_local * span, LANES))
-    out = out_ref.reshape(x_local * span, depth)
-    partial = partial_ref.reshape(x_local * span, depth)
-    height = min(512, x_local * span)
-    for m in range(x_local * span // height):
-        rows = slice(m * height, (m + 1) * height)
-        high, low = interleaved_rows(turned, rows)
-        total = lax.dot_general(
-            jnp.concatenate([high, high, low], axis=1), table[...], (((1,), (0,)), ((), ())), preferred_element_type=f32
+    sources = [
+        part.at[pl.ds(c * depth + early * devices, count), :] for part in (high, low) for c in range(2)
+    ]
+    for n, source in enumerate(sources):
+        pltpu.make_async_copy(source, parts.at[n], tables_in).start()
+
+    def fetch(group):
+        copies = [
+            pltpu.make_async_copy(back.at[pl.ds(early, tail), :, group], lines.at[group], lines_in.at[group])
+        ]
+        if early:
+            at = pl.ds(group * span, span)
+            copies.append(pltpu.make_async_copy(partial.at[:, at, :], cells.at[group], cells_in.at[group]))
+        return copies
+
+    for group in range(groups):
+        for copy in fetch(group):
+            copy.start()
+    pltpu.make_async_copy(parts, parts, tables_in).wait()
+    for n, part in enumerate((parts[0], -parts[1], parts[2], -parts[3], parts[0], -parts[1])):
+        table[n * count : (n + 1) * count, :] = part
+    row_count = count * 2 * GROUP
+    cell_count = x_local * span
+    all_lines = lines.reshape(groups * row_count, LANES)
+    all_cells = cells.reshape(groups * cell_count, depth)
+    height = min(512, cell_count)
+
+    def one(group, _):
+        pltpu.make_async_copy(lines.at[group], lines.at[group], lines_in.at[group]).wait()
+        interleave(
+            all_lines, count, x_local, span, turned.reshape(turned.shape[0] * cell_count, LANES), group * row_count
         )
-        out[rows, :] = total + partial[rows, :] if has_partial else total
+        if early:
+            pltpu.make_async_copy(cells.at[group], cells.at[group], cells_in.at[group]).wait()
+        for m in range(cell_count // height):
+            high, low = interleaved_rows(turned, slice(m * height, (m + 1) * height))
+            total = lax.dot_general(
+                jnp.concatenate([high, high, low], axis=1),
+                table[...],
+                (((1,), (0,)), ((), ())),
+                preferred_element_type=f32,
+            )
+            rows = pl.ds(pl.multiple_of(group * cell_count + m * height, height), height)
+            all_cells[rows, :] = total + all_cells[rows, :] if early else total
+        pltpu.make_async_copy(
+            cells.at[group], out.at[:, pl.ds(pl.multiple_of(group * span, span), span), :], cells_out
+        ).start()
+        return 0
+
+    lax.fori_loop(0, groups, one, 0)
+    pltpu.make_async_copy(cells, cells, cells_out).wait()
 
 
 def on_device(density_one, density_two):
@@ -376,13 +440,15 @@
         pltpu.VMEM((grid_y, 2 * grid_x), bf16),
         pltpu.VMEM((devices, groups, 2 * GROUP, LANES), f32),
         pltpu.VMEM((2, devices, groups, 2 * GROUP, LANES), f32),
-        pltpu.VMEM((max(1, early), devices, 2 * GROUP, LANES), f32),
+        pltpu.VMEM((2, max(1, early), devices, 2 * GROUP, LANES), f32),
         pltpu.VMEM((2, max(1, early) * devices * 2, depth), bf16),
         pltpu.VMEM((max(1, early) * devices * 2 // LANES, x_local * span, LANES), f32),
-        pltpu.VMEM((x_local, span, depth), f32),
+        pltpu.VMEM((2, x_local, span, depth), f32),
         pltpu.SemaphoreType.DMA,
         pltpu.SemaphoreType.DMA((groups + 2 * slices,)),
         pltpu.SemaphoreType.DMA((groups + 2 * slices,)),
+        pltpu.SemaphoreType.DMA((2,)),
+        pltpu.SemaphoreType.DMA((2,)),
     ]
     sizes = (count_x, count_y, x_local, y_local, depth)
     back, partial = pl.pallas_call(
@@ -396,29 +462,24 @@
         ),
     )(density_one, density_two, *(part for length in lengths for part in tables[length]))[:2]
     count = tail * devices
-    cosines = pl.BlockSpec((count, depth), lambda g: (early // tail, 0))
-    sines = pl.BlockSpec((count, depth), lambda g: (depth // count + early // tail, 0))
-    high, low = tables[depth]
-    block = pl.BlockSpec((x_local, span, depth), lambda g: (0, g, 0))
     return pl.pallas_call(
-        functools.partial(depth_inverse_kernel, early > 0),
-        grid=(groups,),
+        functools.partial(depth_inverse_kernel, early),
         out_shape=jax.ShapeDtypeStruct(density_one.shape, f32),
-        in_specs=[
-            pl.BlockSpec((tail, devices, 1, 2 * GROUP, LANES), lambda g: (early // tail, 0, g, 0, 0)),
-            cosines,
-            cosines,
-            sines,
-            sines,
-            block,
+        in_specs=[hbm] * 4,
+        out_specs=hbm,
+        scratch_shapes=[
+            pltpu.VMEM((groups, tail, devices, 2 * GROUP, LANES), f32),
+            pltpu.VMEM((groups, x_local, span, depth), f32),
+            pltpu.VMEM((2 * count // LANES, x_local * span, LANES), f32),
+            pltpu.VMEM((4, count, depth), bf16),
+            pltpu.VMEM((6 * count, depth), bf16),
+            pltpu.SemaphoreType.DMA,
+            pltpu.SemaphoreType.DMA((groups,)),
+            pltpu.SemaphoreType.DMA((groups,)),
+            pltpu.SemaphoreType.DMA,
         ],
-        out_specs=block,
-        scratch_shapes=[
-            pltpu.VMEM((2 * count // LANES, x_local * span, LANES), f32),
-            pltpu.VMEM((6 * count, depth), bf16),
-        ],
-        compiler_params=pltpu.CompilerParams(vmem_limit_bytes=48 * 2**20),
-    )(back, high, low, high, low, partial)
+        compiler_params=pltpu.CompilerParams(vmem_limit_bytes=60 * 2**20),
+    )(back, *tables[depth], partial)
 
 
 def solution(mesh):

time: 1120 us -> 1120 us (level)
  no operation moved by 1% of the time
where the time goes in v3:
time: 1120 us; the launch traced here: 1110 us
  Pallas kernels  1110 us (99%)
    pallas_call x1, Pallas kernels, on_device(): pl.pallas_call(functools.partial(exchange_kernel, sizes), out_shape=[pack...  1090 us

profile of v3, /device:TPU:0, one launch (start us, length us, event | category | flops | bytes accessed | tf_op | source)
XLA Modules:
  0.0 1110.2 jit_solution(3817336974436402642)
XLA Ops:
  0.0 1094.8 %shard_map.37 = (f32[8,32,8,16,128]{4,3,2,1,0:T(8,128)}, f32[128,64,512]{2,1,0:T(8,128)}, f32[8,32,8,16,128]{4,3,2,1,0:T(8,128)}, f32[8,32,8,16,128]{4,3,2,1,0:T...) custom-call(f32[128,64,512]{2,1,0:T(8,128)} %refs_0_.1, ...), custom_call_target="tpu_custom_call" | custom-call | tf_op jit(solution)/shard_map/pallas_call | solution.py:454
  1094.8 15.4 %shard_map.38 = f32[128,64,512]{2,1,0:T(8,128)} custom-call(f32[8,32,8,16,128]{4,3,2,1,0:T(8,128)} %get-tuple-element.7.back, bf16[1024,512]{1,0:T(8,128)(2,1)} %constant.3.refs_2_.high, bf16[1024,512]{1,0:T(8,128)(2,1)} %constant.6.refs_3_.low, f32[128,64,512]{2,1,0:T(8,128)} %get-tuple-element.8.partial), custom_call_target="tpu_custom_call" | custom-call | tf_op jit(solution)/shard_map/pallas_call | solution.py:465
